TPU v7x, 256 devices: a whole 4x4x8 slice. The times are simulated.
256 devices in a mesh: dp: 8 (over z_lo, core), fsdp: 32 (over y, x, z_hi).
Axes of the slice: x: 4, y: 4, z: 8 (z_hi: 2, z_lo: 4; z = z_hi * 4 + z_lo), core: 2. Of those that a mesh axis runs over, the one named last changes fastest.
Arguments:
- hidden_states: bfloat16 [1024, 4096], P(('dp', 'fsdp')), may hold values from -400 to 400
- token_ids: int32 [1024], P(('dp', 'fsdp')), may hold values from 0 to 4095
- norm_gain: float32 [4096], replicated, may hold values from 0.5 to 1.5
- ref_gate_w: bfloat16 [4096, 14784], P('dp', 'fsdp'), may hold values from -0.1875 to 0.1875
- ref_up_w: bfloat16 [4096, 14784], P('dp', 'fsdp'), may hold values from -0.1875 to 0.1875
- ref_down_w: bfloat16 [14784, 4096], P('fsdp', 'dp'), may hold values from -0.09375 to 0.09375
- pol_gate_w: bfloat16 [4096, 14784], P('dp', 'fsdp'), may hold values from -0.1875 to 0.1875
- pol_up_w: bfloat16 [4096, 14784], P('dp', 'fsdp'), may hold values from -0.1875 to 0.1875
- pol_down_w: bfloat16 [14784, 4096], P('fsdp', 'dp'), may hold values from -0.09375 to 0.09375
- sample_lengths: int32 [8, 32], P('dp'), may hold values from 1 to 24, 128 in all within a row
- prompt_index: int32 [8, 32], P('dp'), may hold values from 0 to 3, as said below
- rewards: float32 [8, 32], P('dp'), may hold values from -6 to 6
Outputs:
- grad_gate: float32 [4096, 14784], P('dp', 'fsdp')
- grad_up: float32 [4096, 14784], P('dp', 'fsdp')
- grad_down: float32 [14784, 4096], P('fsdp', 'dp')
- advantage: float32 [8, 32], P('dp')
Inputs may be any that keep to these rules, and one draw needn't show every extreme that they name: `prompt_index`: in each row, every prompt from 0 to 3 is answered by exactly 8 samples. `sample_lengths`: each row sums to 128.
All inputs are finite; a program needn't handle non-finite values.
Results may differ from a plain program's by a relative error of at most 0.013.
Values may be sent and summed in bfloat16 or wider, within the bound.
A program may use at most 64 MiB of HBM per device.

v0:
```python
import jax
import jax.numpy as jnp
from jax import lax
from jax.sharding import PartitionSpec as P

K = 8


EPSILON = 1e-06
KL_WEIGHT = 0.05


def cut_along(shard, dim, count):
    lengths = shard.shape
    tiles = shard.reshape(*lengths[:dim], count, lengths[dim] // count, *lengths[dim + 1 :])
    return jnp.moveaxis(tiles, dim, 0)


def sent_and_summed(shard, axis, dim):
    tiles = cut_along(shard, dim, lax.axis_size(axis))
    arrived = lax.all_to_all(tiles, axis, split_axis=0, concat_axis=0, tiled=True)
    return arrived.sum(axis=0)


def copy_for_each(shard, axis):
    copies = jnp.broadcast_to(shard, (lax.axis_size(axis), *shard.shape))
    return lax.all_to_all(copies, axis, split_axis=0, concat_axis=0, tiled=True)


def laid_out(tiles, dim):
    lengths = list(tiles.shape[1:])
    lengths[dim] *= tiles.shape[0]
    return jnp.moveaxis(tiles, 0, dim).reshape(lengths)


def gather_directly(shard, axis, dim):
    tiles = copy_for_each(shard, axis)
    return laid_out(tiles, dim)


def all_in_one(shard, axis):
    leaves = jax.tree.leaves(shard)
    sequence = sorted(range(len(leaves)), key=lambda k: -leaves[k].size)
    width = (1, *leaves[sequence[0]].shape)[-1]
    lines = [
        jnp.pad(leaves[k].reshape(-1), (0, -leaves[k].size % width)).reshape(-1, width)
        for k in sequence
    ]
    both, at, found = (copy_for_each(jnp.concatenate(lines), axis), 0, {})
    for k, line in zip(sequence, lines):
        slab = both[:, at : at + len(line)].reshape(len(both), -1)
        found[k] = slab[:, : leaves[k].size].reshape(-1, *leaves[k].shape)
        at += len(line)
    numbers = iter(range(len(leaves)))
    return jax.tree.map(lambda _: found[next(numbers)], shard)


def joined_by_halves(pieces, combine):
    while len(jax.tree.leaves(pieces)[0]) > 1:
        pieces = jax.vmap(combine)(
            *(jax.tree.map(lambda part: part[side::2], pieces) for side in (0, 1))
        )
    return jax.tree.map(lambda part: part[0], pieces)


def joined_all(shard, axis, combine):
    pieces = all_in_one(shard, axis)
    return joined_by_halves(pieces, combine)


def taken_together(shard, axis):
    return copy_for_each(shard, axis).sum(axis=0)


def normalize(states, norm_gain):
    values = states.astype(jnp.float32)
    factor = lax.rsqrt(jnp.mean(values * values, axis=-1, keepdims=True) + EPSILON)
    return (values * factor * norm_gain).astype(jnp.bfloat16)


def combine_totals(first, second):
    row_peak = jnp.maximum(first[0], second[0])
    summed = first[1] * jnp.exp(first[0] - row_peak) + second[1] * jnp.exp(second[0] - row_peak)
    return (row_peak, summed, first[2] + second[2])


def grouped_product(left_rows, right_rows, groups, members):
    group_depth = left_rows.shape[0] // (groups * members)
    left_four = left_rows.reshape(members, groups, group_depth, left_rows.shape[1])
    right_four = right_rows.reshape(members, groups, group_depth, right_rows.shape[1])
    terms = jnp.einsum("jgta,jgtb->gab", left_four, right_four, preferred_element_type=jnp.float32)
    rounded = lax.optimization_barrier(terms.astype(jnp.bfloat16))
    return jnp.sum(rounded.astype(jnp.float32), axis=0)


def column_section(normed_cols, state_cols, ids_all, weight_sets, group_index):
    col_width = state_cols.shape[1]
    unit_count = weight_sets[0][0].shape[1]
    in_weights = jnp.concatenate(
        [matrix for triple in weight_sets for matrix in triple[:2]], axis=1
    )
    pre_sums = sent_and_summed(
        jnp.dot(normed_cols, in_weights, preferred_element_type=jnp.float32), "dp", 0
    )
    activations = []
    for model_index in range(len(weight_sets)):
        gate_pre = pre_sums[:, 2 * model_index * unit_count : (2 * model_index + 1) * unit_count]
        up_pre = pre_sums[
            :, (2 * model_index + 1) * unit_count : (2 * model_index + 2) * unit_count
        ]
        activations.append(jax.nn.silu(gate_pre) * up_pre)
    hidden_local = jnp.concatenate(activations, axis=1).astype(jnp.bfloat16)
    hidden_all = gather_directly(hidden_local, "dp", 0)

    def project_out():
        pieces = [
            jnp.dot(
                hidden_all[:, model_index * unit_count : (model_index + 1) * unit_count],
                weight_sets[model_index][2],
                preferred_element_type=jnp.float32,
            )
            for model_index in range(len(weight_sets))
        ]
        return jnp.concatenate(pieces, axis=1)

    out_cols = sent_and_summed(project_out(), "fsdp", 0)
    states = state_cols.astype(jnp.float32)
    col_ids = jnp.arange(col_width, dtype=jnp.int32) + group_index * col_width
    logits_list = []
    peaks = []
    sums = []
    picks = []
    for model_index in range(len(weight_sets)):
        logits = states + out_cols[:, model_index * col_width : (model_index + 1) * col_width]
        row_peak = jnp.max(logits, axis=1)
        logits_list.append(logits)
        peaks.append(row_peak)
        sums.append(jnp.sum(jnp.exp(logits - row_peak[:, None]), axis=1))
        picks.append(jnp.sum(jnp.where(col_ids[None, :] == ids_all[:, None], logits, 0.0), axis=1))
    row_peak, summed, picked = joined_all(
        (jnp.stack(peaks, axis=1), jnp.stack(sums, axis=1), jnp.stack(picks, axis=1)),
        "dp",
        combine_totals,
    )
    log_total = row_peak + jnp.log(summed)
    return (pre_sums, hidden_all, logits_list, log_total, picked - log_total)


def leave_one_out(log_gap, inside, prompt_index, rewards):
    divergence = taken_together(jnp.sum(log_gap[:, None] * inside, axis=0), "fsdp")
    scores = rewards[0] - KL_WEIGHT * divergence
    same_prompt = (prompt_index[0][:, None] == prompt_index[0][None, :]).astype(jnp.float32)
    others = jnp.sum(same_prompt * scores[None, :], axis=1) - scores
    advantage = scores - others / (K - 1)
    weight = jnp.sum(inside * advantage[None, :], axis=1)
    return (advantage, weight)


def local(
    hidden_states,
    token_ids,
    norm_gain,
    ref_gate_w,
    ref_up_w,
    ref_down_w,
    pol_gate_w,
    pol_up_w,
    pol_down_w,
    sample_lengths,
    prompt_index,
    rewards,
):
    token_count = hidden_states.shape[0]
    groups = lax.axis_size("dp")
    members = lax.axis_size("fsdp")
    group_index = lax.axis_index("dp")
    member_index = lax.axis_index("fsdp")
    unit_count = pol_gate_w.shape[1]
    normed = normalize(hidden_states, norm_gain)
    normed_mixed, state_cols = (
        lax.all_to_all(normed, "dp", split_axis=1, concat_axis=0, tiled=True),
        lax.all_to_all(hidden_states, "dp", split_axis=1, concat_axis=0, tiled=True),
    )
    normed_cols = lax.all_gather(normed_mixed, "fsdp", axis=0, tiled=True)
    ids_all = gather_directly(token_ids, "dp", 0)
    own_start = group_index * token_count
    position = member_index * token_count + jnp.arange(token_count, dtype=jnp.int32)
    sample_ends = jnp.cumsum(sample_lengths[0])
    sample_starts = sample_ends - sample_lengths[0]
    inside = (
        (position[:, None] >= sample_starts[None, :]) & (position[:, None] < sample_ends[None, :])
    ).astype(jnp.float32)
    pre_sums, hidden_all, logits_list, log_total, logprob = column_section(
        normed_cols,
        state_cols,
        ids_all,
        [(ref_gate_w, ref_up_w, ref_down_w), (pol_gate_w, pol_up_w, pol_down_w)],
        group_index,
    )
    ref_own = lax.dynamic_slice_in_dim(logprob[:, 0], own_start, token_count, 0)
    pol_own = lax.dynamic_slice_in_dim(logprob[:, 1], own_start, token_count, 0)
    advantage, weight = leave_one_out(pol_own - ref_own, inside, prompt_index, rewards)
    weight_all = gather_directly(weight, "dp", 0)
    col_width = state_cols.shape[1]
    col_ids = jnp.arange(col_width, dtype=jnp.int32) + group_index * col_width
    onehot_cols = (col_ids[None, :] == ids_all[:, None]).astype(jnp.float32)
    grad_cols = (
        -weight_all[:, None] * (onehot_cols - jnp.exp(logits_list[1] - log_total[:, 1:2]))
    ).astype(jnp.bfloat16)
    grad_cols_all = lax.all_gather(grad_cols, "fsdp", axis=0, tiled=True)
    pol_hidden = hidden_all[:, unit_count : 2 * unit_count]
    grad_down = grouped_product(pol_hidden, grad_cols_all, groups, members)
    grad_hidden = sent_and_summed(
        lax.dot_general(
            grad_cols_all, pol_down_w, (((1,), (1,)), ((), ())), preferred_element_type=jnp.float32
        ),
        "dp",
        0,
    )
    gate_pre = pre_sums[:, 2 * unit_count : 3 * unit_count]
    up_pre = pre_sums[:, 3 * unit_count : 4 * unit_count]
    sigmoid_gate = jax.nn.sigmoid(gate_pre)
    grad_gate_pre = grad_hidden * up_pre * sigmoid_gate * (1.0 + gate_pre * (1.0 - sigmoid_gate))
    grad_up_pre = grad_hidden * gate_pre * sigmoid_gate
    gate_grads = jnp.concatenate(
        [grad_gate_pre.astype(jnp.bfloat16), grad_up_pre.astype(jnp.bfloat16)], axis=1
    )
    gate_grads_all = gather_directly(gate_grads, "dp", 0)
    grad_inner = grouped_product(normed_cols, gate_grads_all, groups, members)
    return (grad_inner[:, :unit_count], grad_inner[:, unit_count:], grad_down, advantage[None, :])


def solution(mesh):
    return jax.shard_map(
        local,
        mesh=mesh,
        in_specs=(
            P(("dp", "fsdp"), None),
            P(("dp", "fsdp")),
            P(),
            P("dp", "fsdp"),
            P("dp", "fsdp"),
            P("fsdp", "dp"),
            P("dp", "fsdp"),
            P("dp", "fsdp"),
            P("fsdp", "dp"),
            P("dp", None),
            P("dp", None),
            P("dp", None),
        ),
        out_specs=(P("dp", "fsdp"), P("dp", "fsdp"), P("fsdp", "dp"), P("dp", None)),
        check_vma=False,
    )
```

profile of v0, /device:TPU:1, one launch (start us, length us, event | category | flops | bytes accessed | tf_op | source)
XLA Modules:
  0.0 705.4 jit_solution(487625159166085097)
XLA Ops:
  7.2 1.0 fusion.7
  8.2 0.9 fusion.9
  9.0 12.2 %all_to_all.80 = bf16[4,8,512]{2,0,1:T(4,128)(2,1)S(1)} all-to-all(bf16[4,8,512]{2,0,1:T(4,128)(2,1)S(1)} %bitcast.86), channel_id=1, replica_groups=mesh['dp'=8,'fsdp'=32] {'dp'}, dimensions={1} | all-to-all | bytes 65536 | tf_op jit(solution)/shard_map/all_to_all | solution.py:181
  21.2 0.6 all_to_all.57
  21.9 8.4 %concatenate.16 = bf16[512,1848]{0,1:T(8,128)(2,1)S(1)} concatenate(bf16[512,462]{0,1:T(8,128)(2,1)} %param.15, bf16[512,462]{0,1:T(8,128)(2,1)} %param.16, bf16[512,462]{0,1:T(8,128)(2,1)} %param.18, bf16[512,462]{0,1:T(8,128)(2,1)} %param.19), dimensions={1} | concatenate | bytes 3784704 | tf_op jit(solution)/shard_map/concatenate | solution.py:99
  30.3 72.1 %all-gather.3.cloned.1.call-done = bf16[1024,512]{1,0:T(8,128)(2,1)} async-done(((bf16[32,512]{1,0:T(8,128)(2,1)}), bf16[1024,512]{1,0:T(8,128)(2,1)}) %all-gather.3.cloned.1.call-update) | async-done | bytes 1048592 | tf_op jit(solution)/shard_map/all_gather | solution.py:184
  102.4 3.4 convolution_bitcast_fusion
  106.3 171.0 %all_to_all.81 = f32[8,128,1848]{1,2,0:T(8,128)} all-to-all(f32[8,128,1848]{1,2,0:T(8,128)S(1)} %bitcast.77), channel_id=1, replica_groups=mesh['dp'=8,'fsdp'=32] {'dp'}, dimensions={0} | all-to-all | bytes 15138816 | tf_op jit(solution)/shard_map/all_to_all | solution.py:21
  277.3 3.6 reduce_sum.129
  281.4 47.5 %all_to_all.82 = bf16[8,128,924]{1,2,0:T(8,128)(2,1)S(1)} all-to-all(bf16[8,128,924]{1,2,0:T(8,128)(2,1)S(1)} %broadcast_in_dim.17), channel_id=1, replica_groups=mesh['dp'=8,'fsdp'=32] {'dp'}, dimensions={0} | all-to-all | bytes 3784704 | tf_op jit(solution)/shard_map/all_to_all | solution.py:27
  328.9 0.6 broadcast_in_dim.18
  329.5 4.0 all-to-all-start.5
  333.5 0.7 copy.106
  334.3 0.6 copy.93
  334.9 2.1 fusion.27
  337.0 0.8 fusion.4
  338.3 4.6 all-to-all-start.1
  342.9 4.1 pad_maximum_fusion
  347.0 5.3 copy.74
  352.4 5.0 all-to-all-start.4
  358.2 0.7 reduce.10
  359.0 102.3 %all-to-all-done.4 = f32[32,32,1024]{2,1,0:T(8,128)} async-done(((f32[32,32,1024]{2,1,0:T(8,128)}), f32[32,32,1024]{2,1,0:T(8,128)}, u32[]{:S(2)}, u32[]{:S(2)}) %all-to-all-start.4) | async-done | bytes 4194336 | tf_op jit(solution)/shard_map/all_to_all | solution.py:21
  461.2 2.4 reduce_sum.130
  464.3 0.6 broadcast_in_dim.20
  464.9 4.9 all-to-all-start.6
  469.9 4.9 all-to-all-done.6
  475.1 21.5 %all_to_all.83 = f32[32,1,32]{2,1,0:T(1,128)S(1)} all-to-all(f32[32,1,32]{2,1,0:T(1,128)S(1)} %broadcast_in_dim.21), channel_id=1, replica_groups=mesh['dp'=8,'fsdp'=32] {'fsdp'}, dimensions={0} | all-to-all | bytes 8192 | tf_op jit(solution)/shard_map/all_to_all | solution.py:27
  497.0 0.6 broadcast_in_dim.22
  497.6 5.3 all-to-all-start.8
  502.9 4.8 all-to-all-done.8
  507.9 0.7 fusion.14
  508.6 74.4 %all-gather.5.cloned.1.call-done = bf16[1024,512]{1,0:T(8,128)(2,1)} async-done(((bf16[32,512]{1,0:T(8,128)(2,1)}), bf16[1024,512]{1,0:T(8,128)(2,1)}) %all-gather.5.cloned.1.call-update) | async-done | bytes 1048592 | tf_op jit(solution)/shard_map/all_gather | solution.py:210
  583.0 1.9 fusion.34
  585.9 49.0 %all_to_all.84 = f32[8,128,462]{1,2,0:T(8,128)S(1)} all-to-all(f32[8,128,462]{1,2,0:T(8,128)S(1)} %copy.76), channel_id=1, replica_groups=mesh['dp'=8,'fsdp'=32] {'dp'}, dimensions={0} | all-to-all | bytes 3784704 | tf_op jit(solution)/shard_map/all_to_all | solution.py:21
  635.2 1.5 broadcast_in_dim.44
  636.7 5.2 all-to-all-start.10
  641.9 1.1 reshape.111
  643.3 0.5 copy.81
  643.8 1.2 reshape.118
  645.0 1.1 reshape.119
  646.6 3.6 bitcast_convert_fusion.1
  650.2 1.5 convert_reduce_fusion.1
  651.7 34.2 %all-to-all-done.10 = bf16[8,128,924]{1,2,0:T(8,128)(2,1)} async-done(((bf16[8,128,924]{1,2,0:T(8,128)(2,1)}), bf16[8,128,924]{1,2,0:T(8,128)(2,1)}, u32[]{:S(2)}, u32[]{:S(2)}) %all-to-all-start.10) | async-done | bytes 1892384 | tf_op jit(solution)/shard_map/all_to_all | solution.py:27
  685.9 2.8 copy.78
  688.7 2.2 reshape_reshape.3
  690.9 5.0 bitcast_convert_fusion
  696.0 1.1 convert_reduce_fusion
  697.1 1.5 fusion.31
  (76 shorter events, 5.9 us)
Async XLA Ops:
  7.2 327.7 %copy-start = (bf16[462,512]{1,0:T(8,128)(2,1)S(1)}, bf16[462,512]{1,0:T(8,128)(2,1)}, u32[]{:S(2)}) copy-start(bf16[462,512]{1,0:T(8,128)(2,1)} %param.20) | copy-start | bytes 1419268
  7.2 95.2 %all-gather.3.cloned.1.call-start = ((), (), s32[]{:S(2)}) async-start(), calls=%async_computation.11 | async-start | bytes 1081344 | tf_op jit(solution)/shard_map/all_gather | solution.py:184
  281.4 47.5 %copy-start.9 = (s32[4]{0:T(128)S(1)}, s32[4]{0:T(128)}, u32[]{:S(2)}) copy-start(s32[4]{0:T(128)} %param.13) | copy-start | bytes 52
  329.5 8.8 %all-to-all-start.5 = ((s32[8,1,4]{2,1,0:T(1,128)}), s32[8,1,4]{2,1,0:T(1,128)S(1)}, u32[]{:S(2)}, u32[]{:S(2)}) async-start(s32[8,1,4]{2,1,0:T(1,128)} %broadcast_in_dim.18), calls=%async_computation.5 | async-start | bytes 8192 | tf_op jit(solution)/shard_map/all_to_all | solution.py:27
  334.9 2.1 copy-start.2
  334.9 2.1 copy-start.7
  338.3 14.0 %all-to-all-start.1 = ((bf16[4,8,512]{2,0,1:T(4,128)(2,1)}), bf16[4,8,512]{2,0,1:T(4,128)(2,1)S(1)}, u32[]{:S(2)}, u32[]{:S(2)}) async-start(bf16[4,8,512]{2,0,1:T(4,128)(2,1)} %bitcast.4), calls=%async_computation.1 | async-start | bytes 65536 | tf_op jit(solution)/shard_map/all_to_all | solution.py:182
  352.4 5.0 copy-start.10
  352.4 108.9 %all-to-all-start.4 = ((f32[32,32,1024]{2,1,0:T(8,128)}), f32[32,32,1024]{2,1,0:T(8,128)}, u32[]{:S(2)}, u32[]{:S(2)}) async-start(f32[32,32,1024]{2,1,0:T(8,128)} %bitcast.78), calls=%async_computation.4 | async-start | bytes 8388608 | tf_op jit(solution)/shard_map/all_to_all | solution.py:21
  359.0 137.7 %copy-start.11 = (f32[1,32]{1,0:T(1,128)S(1)}, f32[1,32]{1,0:T(1,128)}, u32[]{:S(2)}) copy-start(f32[1,32]{1,0:T(1,128)} %param.23) | copy-start | bytes 388
  359.0 137.7 %copy-start.8 = (s32[1,32]{1,0:T(1,128)S(1)}, s32[1,32]{1,0:T(1,128)}, u32[]{:S(2)}) copy-start(s32[1,32]{1,0:T(1,128)} %param.22) | copy-start | bytes 388
  464.9 9.8 %all-to-all-start.6 = ((f32[8,96,2]{1,2,0:T(2,128)}), f32[8,96,2]{1,2,0:T(2,128)S(1)}, u32[]{:S(2)}, u32[]{:S(2)}) async-start(f32[8,96,2]{1,2,0:T(2,128)} %broadcast_in_dim.20), calls=%async_computation.6 | async-start | bytes 16384 | tf_op jit(solution)/shard_map/all_to_all | solution.py:27
  496.9 88.5 %copy-start.12 = (f32[1,32]{1,0:T(1,128)}, f32[1,32]{1,0:T(1,128)S(1)}, u32[]{:S(2)}) copy-start(f32[1,32]{1,0:T(1,128)S(1)} %fusion.24) | copy-start | bytes 388
  497.6 10.2 %all-to-all-start.8 = ((f32[8,1,4]{2,1,0:T(1,128)}), f32[8,1,4]{2,1,0:T(1,128)S(1)}, u32[]{:S(2)}, u32[]{:S(2)}) async-start(f32[8,1,4]{2,1,0:T(1,128)} %broadcast_in_dim.22), calls=%async_computation.8 | async-start | bytes 8192 | tf_op jit(solution)/shard_map/all_to_all | solution.py:27
  502.9 80.1 %all-gather.5.cloned.1.call-start = ((), (), s32[]{:S(2)}) async-start(), calls=%async_computation.12 | async-start | bytes 1081344 | tf_op jit(solution)/shard_map/all_gather | solution.py:210
  636.7 5.2 copy-start.5
  636.7 6.3 copy-start.3
  636.7 49.2 %all-to-all-start.10 = ((bf16[8,128,924]{1,2,0:T(8,128)(2,1)}), bf16[8,128,924]{1,2,0:T(8,128)(2,1)}, u32[]{:S(2)}, u32[]{:S(2)}) async-start(bf16[8,128,924]{1,2,0:T(8,128)(2,1)} %broadcast_in_dim.44), calls=%async_computation.10 | async-start | bytes 3801088 | tf_op jit(solution)/shard_map/all_to_all | solution.py:27
  643.2 1.7 copy-start.4
  645.0 1.6 copy-start.6
  696.0 2.6 copy-start.1
Sparse Core Ops, SparseCore 0:
  22.0 80.3 all-gather.2
  508.7 74.2 all-gather.4
where the time goes:
time: 707 us; the launch traced here: 705 us
  blocking collectives  301 us (43%)
  waiting for transfers between devices  293 us (41%)
  local copies, waits for them, and re-layouts  32.9 us (5%)
  starting transfers between devices  29.1 us (4%)
  other arithmetic  17.8 us (3%)
  matrix products  16.8 us (2%)
  between operations  14.4 us (2%)
    all_to_all x2, blocking collectives, sent_and_summed(): lax.all_to_all(tiles, axis, split_axis=0, concat_axis=0, tiled=True)  220 us
    all_to_all x1, waiting for transfers between devices, sent_and_summed(): lax.all_to_all(tiles, axis, split_axis=0, concat_axis=0, tiled=True)  102 us
    all_gather x1, waiting for transfers between devices, local(): grad_cols_all = lax.all_gather(grad_cols, 'fsdp', axis=0, tiled=True)  74.4 us
    all_gather x1, waiting for transfers between devices, local(): normed_cols = lax.all_gather(normed_mixed, 'fsdp', axis=0, tiled=True)  72.1 us
    all_to_all x2, blocking collectives, copy_for_each(): return lax.all_to_all(copies, axis, split_axis=0, concat_axis=0, tiled=True)  69 us
    all_to_all x4, waiting for transfers between devices, copy_for_each(): return lax.all_to_all(copies, axis, split_axis=0, concat_axis=0, tiled=True)  44.5 us
    all_to_all x4, starting transfers between devices, copy_for_each(): return lax.all_to_all(copies, axis, split_axis=0, concat_axis=0, tiled=True)  19.4 us
  transfers between devices with their start and end apart: 8, of which 7 were waited for; matrix products, arithmetic and copies ran while one was open for 5% of the time, Pallas kernels for 0%

commit v1 on v0

v1 whole, which is shorter than its diff:
```python
import functools
from types import SimpleNamespace

import jax
import jax.numpy as jnp
from jax import lax
from jax.experimental import pallas as pl
from jax.experimental.pallas import tpu as pltpu
from jax.sharding import PartitionSpec as P

K = 8
EPSILON = 1e-06
KL_WEIGHT = 0.05

F32 = jnp.float32
BF16 = jnp.bfloat16
DMA = pltpu.SemaphoreType.DMA
VMEM = pl.BlockSpec(memory_space=pltpu.VMEM)

LANES = 128
PLANE = 16
CHIPS = 4
SKEW = 2


def copy_to(src, dst, send, recv, **where):
    return pltpu.make_async_remote_copy(
        src_ref=src,
        dst_ref=dst,
        send_sem=send,
        recv_sem=recv,
        device_id=where,
        device_id_type=pl.DeviceIdType.MESH,
    )


def signal(**where):
    pl.semaphore_signal(
        pltpu.get_barrier_semaphore(),
        inc=1,
        device_id=where,
        device_id_type=pl.DeviceIdType.MESH,
    )


def each(start, stop, body):
    def step(index, carry):
        body(index)
        return carry

    lax.fori_loop(start, stop, step, 0)


def greet_all(me, groups, member):
    plane, half = member // 2, member % 2
    mate = member + 1 - 2 * half

    def row(step):
        signal(dp=lax.rem(me + step, groups))

    def flat(step):
        signal(fsdp=lax.rem(plane + step, PLANE) * 2 + half)

    each(1, groups, row)
    each(1, PLANE, flat)
    signal(fsdp=mate)
    pl.semaphore_wait(pltpu.get_barrier_semaphore(), groups - 1 + PLANE - 1 + 1)


def row_exchange(me, groups, sent, landed, send, recv):
    def copy(step):
        peer = lax.rem(me + step, groups)
        return copy_to(sent(peer), landed(me), send.at[step], recv.at[me], dp=peer)

    def wait(step):
        source = lax.rem(me + groups - step, groups)
        copy_to(sent(source), landed(source), send.at[step], recv.at[source], dp=source).wait_recv()

    return (
        lambda: each(1, groups, lambda step: copy(step).start()),
        lambda: each(1, groups, wait),
        lambda: each(1, groups, lambda step: copy(step).wait_send()),
    )


def plane_gather(member, views, mate_send, mate_recv, send, recv, meanwhile=lambda: None):
    plane, half = member // 2, member % 2
    mate = member + 1 - 2 * half

    def mate_copy(i, block):
        view = views[i](block)
        return copy_to(view, view, mate_send.at[i], mate_recv.at[i], fsdp=mate)

    def flat(i, which, block, step):
        view = views[i](block)
        peer = lax.rem(plane + step, PLANE) * 2 + half
        return copy_to(
            view, view, send.at[i, which, step], recv.at[i, which, plane], fsdp=peer
        )

    def flat_wait(i, which, step):
        source = lax.rem(plane + PLANE - step, PLANE)
        view = views[i](source * 2 + (half if which == 0 else 1 - half))
        copy_to(
            view, view, send.at[i, which, step], recv.at[i, which, source], fsdp=source * 2 + half
        ).wait_recv()

    count = range(len(views))
    for i in count:
        mate_copy(i, member).start()
    each(1, PLANE, lambda step: [flat(i, 0, member, step).start() for i in count])
    meanwhile()
    for i in count:
        mate_copy(i, mate).wait_recv()
    each(1, PLANE, lambda step: [flat(i, 1, mate, step).start() for i in count])
    each(1, PLANE, lambda step: [flat_wait(i, 0, step) for i in count])
    each(1, PLANE, lambda step: [flat_wait(i, 1, step) for i in count])
    for i in count:
        mate_copy(i, member).wait_send()
    each(1, PLANE, lambda step: [flat(i, 0, member, step).wait_send() for i in count])
    each(1, PLANE, lambda step: [flat(i, 1, mate, step).wait_send() for i in count])


def norm_phase(s, groups, me, member):
    count, width = s.rows.shape
    block = width // groups
    values = s.rows[...].astype(F32)
    factor = lax.rsqrt(jnp.mean(values * values, axis=-1, keepdims=True) + EPSILON)
    for d in range(groups):
        s.row_sent[d] = s.rows[:, d * block : (d + 1) * block]
    s.meta_sent[...] = jnp.zeros_like(s.meta_sent)
    small = (s.lengths, s.prompts, s.rewards, s.ids)
    for i, value in enumerate(small):
        s.meta_sent[i : i + 1, 0 : value.shape[1]] = value[...].astype(F32)
    s.meta_sent[4 : 4 + count, :] = jnp.broadcast_to(factor, (count, LANES))
    moves = (
        row_exchange(
            me, groups, lambda p: s.row_sent.at[p], lambda g: s.row_landed.at[g], s.r_send, s.r_recv
        ),
        row_exchange(
            me, groups, lambda p: s.meta_sent, lambda g: s.meta.at[g], s.m_send, s.m_recv
        ),
    )
    for start, _, _ in moves:
        start()
    s.row_landed[me] = s.row_sent[me]
    s.meta[me] = s.meta_sent[...]
    for _, wait, _ in moves:
        wait()
    gain = s.gain[:, pl.ds(pl.multiple_of(me * block, block), block)]
    for g in range(groups):
        state = s.row_landed[g].astype(F32)
        s.states[g * count : (g + 1) * count, :] = state
        s.scaled[g * count : (g + 1) * count, :] = state * s.meta[g, 4 : 4 + count, 0:1] * gain
    rows = groups * count
    view = lambda b: s.normed.at[pl.ds(pl.multiple_of(b * rows, rows), rows), :]
    s.normed[pl.ds(pl.multiple_of(member * rows, rows), rows), :] = s.scaled[...].astype(BF16)

    def columns_of_ids():
        ids = turned([s.meta[g, 3:4, :] for g in range(groups)])
        for g in range(groups):
            s.id_rows[g * count : (g + 1) * count, :] = jnp.broadcast_to(
                ids[0:count, g : g + 1], (count, LANES)
            )

    plane_gather(
        member, (view,), s.n_mate_send, s.n_mate_recv, s.n_send, s.n_recv, columns_of_ids
    )
    for _, _, finish in moves:
        finish()


def run_reduce(steps, skew, me, plane, product, finish, gathered, s, arrived=None):
    chip, core = me // 2, me % 2
    partner = me + 1 - 2 * core
    quarter = s.own.shape[2]
    block = quarter // 4
    chunk = quarter // steps
    per = steps // 4
    lows = s.sent.shape[1] if s.sent is not None else 0
    count = s.own.shape[1]
    pairs = [(s.sent, s.landed, s.pair_send, s.pair_recv)]
    if s.high_sent is not None:
        pairs.append((s.high_sent, s.high_landed, s.high_send, s.high_recv))

    def pair_copies(e):
        return [
            copy_to(a.at[e], b.at[e], send.at[e], recv.at[e], dp=partner)
            for a, b, send, recv in pairs
        ]

    def place(e, c, b):
        return lax.rem(plane + 1 + 4 * b + 2 * e + c, PLANE)

    def left_rows(ref, e, c):
        return jnp.concatenate(
            [
                ref[pl.ds(pl.multiple_of(place(e, c, b) * block, block), block), :]
                for b in range(4)
            ],
            axis=0,
        )

    def first(e):
        left = left_rows(s.left, e, 1 - core)
        for i in range(count):
            if i < lows:
                s.sent[e, i] = product(left, i).astype(s.sent.dtype)
            else:
                s.high_sent[e, i - lows] = product(left, i)
        for copy in pair_copies(e):
            copy.start()

    def second(e):
        left = left_rows(s.left, e, core)
        for i in range(count):
            s.own[e, i] = product(left, i)

    each(0, 2, first)
    each(0, 2, second)

    at = (CHIPS - 1 - chip, chip)
    onward = (me - 2, me + 2)
    backward = (me + 2, me - 2)

    def part(j):
        return pl.ds(pl.multiple_of(j * chunk, chunk), chunk)

    def out_rows(e, c, j):
        start = place(e, c, j // per) * block + (j % per) * chunk
        return pl.ds(pl.multiple_of(start, chunk), chunk)

    def up_copy(e, j):
        return copy_to(
            s.up.at[e, :, part(j), :],
            s.down.at[e, :, part(j), :],
            s.up_send.at[e, j],
            s.up_recv.at[e, j],
            dp=onward[e],
        )

    def back_copy(e, j):
        view = gathered.at[:, out_rows(e, core, j), :]
        return copy_to(view, view, s.back_send.at[e, j], s.back_recv.at[e, j], dp=backward[e])

    def side_copy(e, j, c):
        view = gathered.at[:, out_rows(e, c, j), :]
        return copy_to(view, view, s.side_send.at[e, j], s.side_recv.at[e, j], dp=partner)

    def here(e, j):
        found = []
        for i in range(count):
            if i < lows:
                other = s.landed[e, i, part(j), :].astype(F32)
            else:
                other = s.high_landed[e, i - lows, part(j), :]
            found.append(s.own[e, i, part(j), :] + other)
        return found

    def send_up(e, j, values):
        for i in range(count):
            s.up[e, i, part(j), :] = values[i].astype(BF16)
        up_copy(e, j).start()

    for e in (0, 1):
        for copy in pair_copies(e):
            copy.wait_recv()

        @pl.when(at[e] == 0)
        def _():
            each(0, steps, lambda j: send_up(e, j, here(e, j)))

    def loop(t):
        for e in (0, 1):
            j = t - skew * (at[e] - 1)

            @pl.when((at[e] > 0) & (j >= 0) & (j < steps))
            def _():
                up_copy(e, j).wait_recv()
                total = [
                    value + s.down[e, i, part(j), :].astype(F32)
                    for i, value in enumerate(here(e, j))
                ]

                @pl.when(at[e] < CHIPS - 1)
                def _():
                    send_up(e, j, total)

                @pl.when(at[e] == CHIPS - 1)
                def _():
                    finish(total, part(j), out_rows(e, core, j))
                    back_copy(e, j).start()
                    side_copy(e, j, core).start()

        for e in (0, 1):
            j = t - skew * (2 * CHIPS - 3 - at[e])

            @pl.when((at[e] < CHIPS - 1) & (j >= 0) & (j < steps))
            def _():
                back_copy(e, j).wait_recv()

                @pl.when(at[e] > 0)
                def _():
                    back_copy(e, j).start()

                side_copy(e, j, core).start()

        if arrived is not None:
            for e in (0, 1):
                j = t - skew * (2 * CHIPS - 3 - at[e])

                @pl.when((j >= 0) & (j < steps) & (j % per == per - 1))
                def _():
                    arrived(place(e, core, j // per))

                k = j - 1

                @pl.when((k >= 0) & (k < steps) & (k % per == per - 1))
                def _():
                    each(k - (per - 1), k + 1, lambda i: side_copy(e, i, 1 - core).wait_recv())
                    arrived(place(e, 1 - core, k // per))

    each(0, steps + skew * (2 * CHIPS - 3) + (0 if arrived is None else 1), loop)

    def close(j):
        for e in (0, 1):
            if arrived is None:
                side_copy(e, j, 1 - core).wait_recv()
            side_copy(e, j, core).wait_send()

            @pl.when(at[e] < CHIPS - 1)
            def _():
                up_copy(e, j).wait_send()

            @pl.when(at[e] > 0)
            def _():
                back_copy(e, j).wait_send()

    def finally_():
        each(0, steps, close)
        for e in (0, 1):
            for copy in pair_copies(e):
                copy.wait_send()

    return finally_


def turned(rows_of):
    fill = jnp.zeros((LANES - len(rows_of), LANES), F32)
    return jnp.concatenate([*rows_of, fill], axis=0).T


def advantages(s, groups, members, count):
    lengths, prompts, rewards = (
        jnp.concatenate([s.meta[g, i : i + 1, :] for g in range(groups)], axis=0) for i in range(3)
    )
    before = lax.broadcasted_iota(jnp.int32, (LANES, LANES), 0) <= lax.broadcasted_iota(
        jnp.int32, (LANES, LANES), 1
    )
    ends = jnp.dot(
        lengths.astype(BF16),
        jnp.where(before, 1.0, 0.0).astype(BF16),
        preferred_element_type=F32,
    )
    starts = ends - lengths
    gaps = jnp.concatenate([s.gaps[f, 0:1, :] for f in range(members)], axis=0)
    first = lax.broadcasted_iota(jnp.int32, (members, LANES), 0).astype(F32) * count
    lane = lax.broadcasted_iota(jnp.int32, (members, LANES), 1)

    def inside(g, i):
        position = first + i
        return (position >= starts[g : g + 1, :]) & (position < ends[g : g + 1, :])

    sums = []
    for g in range(groups):
        found = jnp.zeros((members, LANES), F32)
        for i in range(count):
            column = g * count + i
            found += jnp.where(inside(g, i), gaps[:, column : column + 1], 0.0)
        sums.append(jnp.sum(found, axis=0, keepdims=True))
    scores = rewards - KL_WEIGHT * jnp.concatenate(sums, axis=0)
    others = -scores
    for prompt in range(s.lengths.shape[1] // K):
        same = prompts == prompt
        total = jnp.sum(jnp.where(same, scores, 0.0), axis=1, keepdims=True)
        others += jnp.where(same, total, 0.0)
    advantage = scores - others / (K - 1)
    weights = jnp.zeros((members, LANES), F32)
    for g in range(groups):
        for i in range(count):
            mine = jnp.where(inside(g, i), advantage[g : g + 1, :], 0.0)
            weights = jnp.where(
                lane == g * count + i, jnp.sum(mine, axis=1, keepdims=True), weights
            )
    return advantage, weights


def logits_phase(s, groups, members, me, member):
    plane, half = member // 2, member % 2
    mate = member + 1 - 2 * half
    rows, width = s.states.shape
    pair = 2 * rows

    def share(other):
        return copy_to(
            s.l_sent.at[other],
            s.l_landed.at[plane],
            s.l_send.at[other],
            s.l_recv.at[plane],
            fsdp=other * 2 + half,
        )

    def project(other):
        out = [
            jnp.dot(
                s.hidden[m, pl.ds(pl.multiple_of(other * pair, pair), pair), :],
                right[...],
                preferred_element_type=F32,
            )
            for m, right in enumerate((s.ref_down, s.pol_down))
        ]

        @pl.when(other == plane)
        def _():
            for m in (0, 1):
                s.total[m] = out[m]

        @pl.when(other != plane)
        def _():
            for m in (0, 1):
                s.l_sent[other, m] = out[m].astype(BF16)
            share(other).start()

    def rest():
        def add(step):
            source = lax.rem(plane + PLANE - step, PLANE)
            copy_to(
                s.l_sent.at[source],
                s.l_landed.at[source],
                s.l_send.at[source],
                s.l_recv.at[source],
                fsdp=source * 2 + half,
            ).wait_recv()
            s.total[...] += s.l_landed[source].astype(F32)

        each(1, PLANE, add)
        theirs = pl.ds(pl.multiple_of((1 - half) * rows, rows), rows)
        mine = pl.ds(pl.multiple_of(half * rows, rows), rows)
        s.mate_ref[...] = s.total[0, theirs, :].astype(BF16)
        s.mate_pol[...] = s.total[1, theirs, :]
        mate_copies = (
            copy_to(s.mate_ref, s.mate_ref_in, s.h_send.at[0], s.h_recv.at[0], fsdp=mate),
            copy_to(s.mate_pol, s.mate_pol_in, s.h_send.at[1], s.h_recv.at[1], fsdp=mate),
        )
        for copy in mate_copies:
            copy.start()
        s.pol_hidden[...] = s.hidden[1]
        for copy in mate_copies:
            copy.wait_recv()
        logits = [
            s.states[...] + s.total[0, mine, :] + s.mate_ref_in[...].astype(F32),
            s.states[...] + s.total[1, mine, :] + s.mate_pol_in[...],
        ]
        columns = lax.broadcasted_iota(jnp.int32, (rows, width), 1) + me * width
        picked = columns.astype(F32) == s.id_rows[:, 0:1]
        lane = lax.broadcasted_iota(jnp.int32, (rows, LANES), 1)
        tile = jnp.zeros((rows, LANES), F32)
        for m in (0, 1):
            peak = jnp.max(logits[m], axis=1, keepdims=True)
            summed = jnp.sum(jnp.exp(logits[m] - peak), axis=1, keepdims=True)
            pick = jnp.sum(jnp.where(picked, logits[m], 0.0), axis=1, keepdims=True)
            for i, value in enumerate((peak, summed, pick)):
                tile = jnp.where(lane == 3 * m + i, value, tile)
        full = jnp.concatenate([tile, jnp.zeros((LANES - rows, LANES), F32)], axis=0)
        s.stats[...] = full.T[0:8, :]
        start, wait, done = row_exchange(
            me, groups, lambda p: s.stats, lambda g: s.stats_all.at[g], s.s_send, s.s_recv
        )
        start()
        s.stats_all[me] = s.stats[...]
        wait()
        real = lax.broadcasted_iota(jnp.int32, (1, LANES), 1) < rows
        log_totals, logprobs = [], []
        for m in (0, 1):
            peaks = [s.stats_all[g, 3 * m : 3 * m + 1, :] for g in range(groups)]
            peak = functools.reduce(jnp.maximum, peaks)
            summed = sum(
                s.stats_all[g, 3 * m + 1 : 3 * m + 2, :] * jnp.exp(peaks[g] - peak)
                for g in range(groups)
            )
            pick = sum(s.stats_all[g, 3 * m + 2 : 3 * m + 3, :] for g in range(groups))
            log_total = peak + jnp.log(jnp.where(real, summed, 1.0))
            log_totals.append(log_total)
            logprobs.append(pick - log_total)
        s.gaps[member] = jnp.broadcast_to(logprobs[1] - logprobs[0], (8, LANES))
        log_total = turned([log_totals[1]])[0:rows, 0:1]
        grad = jnp.where(picked, 1.0, 0.0) - jnp.exp(logits[1] - log_total)
        s.raw[pl.ds(pl.multiple_of(member * rows, rows), rows), :] = grad.astype(BF16)
        views = (
            lambda b: s.gaps.at[b],
            lambda b: s.raw.at[pl.ds(pl.multiple_of(b * rows, rows), rows), :],
        )
        plane_gather(member, views, s.g_mate_send, s.g_mate_recv, s.g_send, s.g_recv)
        done()
        for copy in mate_copies:
            copy.wait_send()
        each(1, PLANE, lambda step: share(lax.rem(plane + step, PLANE)).wait_send())
        advantage, weights = advantages(s, groups, members, rows // groups)
        s.advantage_rows[...] = advantage
        s.advantage[...] = s.advantage_rows[pl.ds(me, 1), 0 : s.advantage.shape[1]]
        fill = jnp.zeros((LANES - members, LANES), F32)
        turned_weights = jnp.concatenate([weights, fill], axis=0).T
        for f in range(members):
            at = slice(f * rows, (f + 1) * rows)
            s.grads[at, :] = (
                -turned_weights[0:rows, f : f + 1] * s.raw[at, :].astype(F32)
            ).astype(BF16)

    return project, rest


def step_kernel(names, groups, members, forward_steps, backward_steps, skew, *refs):
    s = SimpleNamespace(**dict(zip(names, refs)))
    me, member = lax.axis_index("dp"), lax.axis_index("fsdp")
    plane = member // 2
    greet_all(me, groups, member)
    norm_phase(s, groups, me, member)
    project, rest = logits_phase(s, groups, members, me, member)

    def parts(prefix, left):
        found = {
            name: getattr(s, prefix + name, None)
            for name in RUN_NAMES + ("high_sent", "high_landed", "high_send", "high_recv")
        }
        return SimpleNamespace(left=left, **found)

    weights = (s.ref_gate, s.ref_up, s.pol_gate, s.pol_up)

    def units(left, right):
        return lax.dot_general(
            left, right, (((1,), (1,)), ((), ())), preferred_element_type=F32
        )

    def activate(total, rows, out_rows):
        for m in (0, 1):
            gate, up_value = total[2 * m], total[2 * m + 1]
            s.hidden[m, out_rows, :] = (gate * jax.nn.sigmoid(gate) * up_value).astype(BF16)
        s.pre[0, rows, :] = total[2]
        s.pre[1, rows, :] = total[3]

    close_forward = run_reduce(
        forward_steps,
        skew,
        me,
        plane,
        lambda left, i: units(left, weights[i][...]),
        activate,
        s.hidden,
        parts("f_", s.normed),
        project,
    )
    rest()
    close_forward()

    def differentiate(total, rows, out_rows):
        grad_hidden, gate, up_value = total[0], s.pre[0, rows, :], s.pre[1, rows, :]
        sigmoid = jax.nn.sigmoid(gate)
        s.gates[0, out_rows, :] = (
            grad_hidden * up_value * sigmoid * (1.0 + gate * (1.0 - sigmoid))
        ).astype(BF16)
        s.gates[1, out_rows, :] = (grad_hidden * gate * sigmoid).astype(BF16)

    run_reduce(
        backward_steps,
        skew,
        me,
        plane,
        lambda left, i: units(left, s.pol_down[...]),
        differentiate,
        s.gates,
        parts("b_", s.grads),
    )()


RUN_NAMES = (
    "own",
    "sent",
    "landed",
    "up",
    "down",
    "pair_send",
    "pair_recv",
    "up_send",
    "up_recv",
    "back_send",
    "back_recv",
    "side_send",
    "side_recv",
)


def run_scratch(prefix, count, lows, quarter, units, steps):
    wide = lambda n, kind: pltpu.VMEM((2, n, quarter, units), kind)
    shapes = [wide(count, F32), wide(lows, BF16), wide(lows, BF16)]
    shapes += [wide(count, BF16)] * 2 + [DMA((2,))] * 2 + [DMA((2, steps))] * 6
    found = {prefix + name: shape for name, shape in zip(RUN_NAMES, shapes)}
    if lows < count:
        found[prefix + "high_sent"] = found[prefix + "high_landed"] = wide(count - lows, F32)
        found[prefix + "high_send"] = found[prefix + "high_recv"] = DMA((2,))
    return found


FORWARD_STEPS, BACKWARD_STEPS, SKEW = 16, 8, 3


def one_step(inputs, groups, members):
    count, width = inputs["rows"].shape
    samples = inputs["lengths"].shape[1]
    units = inputs["ref_gate"].shape[0]
    block, rows = width // groups, groups * count
    tokens = members * rows
    quarter = tokens // 4
    shape = jax.ShapeDtypeStruct
    outputs = {
        "normed": shape((tokens, block), BF16),
        "gates": shape((2, tokens, units), BF16),
        "pol_hidden": shape((tokens, units), BF16),
        "grads": shape((tokens, block), BF16),
        "advantage": shape((1, samples), F32),
    }
    gather = lambda n: [DMA((n,)), DMA((n,)), DMA((n, 2, PLANE)), DMA((n, 2, PLANE))]
    scratch = {
        "row_sent": pltpu.VMEM((groups, count, block), BF16),
        "row_landed": pltpu.VMEM((groups, count, block), BF16),
        "meta_sent": pltpu.VMEM((8, LANES), F32),
        "meta": pltpu.VMEM((groups, 8, LANES), F32),
        "states": pltpu.VMEM((rows, block), F32),
        "scaled": pltpu.VMEM((rows, block), F32),
        "id_rows": pltpu.VMEM((rows, LANES), F32),
        **{name: DMA((groups,)) for name in ("r_send", "r_recv", "m_send", "m_recv")},
        **dict(zip(("n_mate_send", "n_mate_recv", "n_send", "n_recv"), gather(1))),
        **run_scratch("f_", 4, 2, quarter, units, FORWARD_STEPS),
        "hidden": pltpu.VMEM((2, tokens, units), BF16),
        "pre": pltpu.VMEM((2, quarter, units), F32),
        "l_sent": pltpu.VMEM((PLANE, 2, 2 * rows, block), BF16),
        "l_landed": pltpu.VMEM((PLANE, 2, 2 * rows, block), BF16),
        "l_send": DMA((PLANE,)),
        "l_recv": DMA((PLANE,)),
        "total": pltpu.VMEM((2, 2 * rows, block), F32),
        "mate_ref": pltpu.VMEM((rows, block), BF16),
        "mate_ref_in": pltpu.VMEM((rows, block), BF16),
        "mate_pol": pltpu.VMEM((rows, block), F32),
        "mate_pol_in": pltpu.VMEM((rows, block), F32),
        "h_send": DMA((2,)),
        "h_recv": DMA((2,)),
        "stats": pltpu.VMEM((8, LANES), F32),
        "stats_all": pltpu.VMEM((groups, 8, LANES), F32),
        "s_send": DMA((groups,)),
        "s_recv": DMA((groups,)),
        "raw": pltpu.VMEM((tokens, block), BF16),
        "gaps": pltpu.VMEM((members, 8, LANES), F32),
        "advantage_rows": pltpu.VMEM((groups, LANES), F32),
        **dict(zip(("g_mate_send", "g_mate_recv", "g_send", "g_recv"), gather(2))),
        **run_scratch("b_", 1, 1, quarter, units, BACKWARD_STEPS),
    }
    names = (*inputs, *outputs, *scratch)
    results = pl.pallas_call(
        functools.partial(
            step_kernel, names, groups, members, FORWARD_STEPS, BACKWARD_STEPS, SKEW
        ),
        out_shape=tuple(outputs.values()),
        in_specs=[VMEM] * len(inputs),
        out_specs=(VMEM,) * len(outputs),
        scratch_shapes=list(scratch.values()),
        compiler_params=pltpu.CompilerParams(collective_id=0, has_side_effects=True),
        name="one_step",
    )(*inputs.values())
    return dict(zip(outputs, results))


def local(
    hidden_states,
    token_ids,
    norm_gain,
    ref_gate_w,
    ref_up_w,
    ref_down_w,
    pol_gate_w,
    pol_up_w,
    pol_down_w,
    sample_lengths,
    prompt_index,
    rewards,
):
    found = one_step(
        {
            "rows": hidden_states,
            "gain": norm_gain.reshape(1, -1),
            "lengths": sample_lengths,
            "prompts": prompt_index,
            "rewards": rewards,
            "ids": token_ids.reshape(1, -1),
            "ref_gate": ref_gate_w.T,
            "ref_up": ref_up_w.T,
            "pol_gate": pol_gate_w.T,
            "pol_up": pol_up_w.T,
            "ref_down": ref_down_w,
            "pol_down": pol_down_w,
        },
        lax.axis_size("dp"),
        lax.axis_size("fsdp"),
    )

    def outer(left, right):
        return lax.dot_general(
            left, right, (((0,), (0,)), ((), ())), preferred_element_type=F32
        )

    return (
        outer(found["normed"], found["gates"][0]),
        outer(found["normed"], found["gates"][1]),
        outer(found["pol_hidden"], found["grads"]),
        found["advantage"],
    )


def solution(mesh):
    return jax.shard_map(
        local,
        mesh=mesh,
        in_specs=(
            P(("dp", "fsdp"), None),
            P(("dp", "fsdp")),
            P(),
            P("dp", "fsdp"),
            P("dp", "fsdp"),
            P("fsdp", "dp"),
            P("dp", "fsdp"),
            P("dp", "fsdp"),
            P("fsdp", "dp"),
            P("dp", None),
            P("dp", None),
            P("dp", None),
        ),
        out_specs=(P("dp", "fsdp"), P("dp", "fsdp"), P("fsdp", "dp"), P("dp", None)),
        check_vma=False,
    )
```

time: 707 us -> 178 us (0.25)
  blocking collectives: 301 us -> 0 us
  waiting for transfers between devices: 293 us -> 0 us
  Pallas kernels: 0 us -> 170 us
  local copies, waits for them, and re-layouts: 32.9 us -> 0.52 us
  starting transfers between devices: 29.1 us -> 0 us
  other arithmetic: 17.8 us -> 0 us
  between operations: 14.4 us -> 0.66 us
  matrix products: 16.8 us -> 6.59 us
    all_to_all x5 -> x0, blocking collectives: 301 us -> none  [the longest x2 220 us: sent_and_summed(): lax.all_to_all(tiles, axis, split_axis=0, concat_axis=0, tiled=True)]
    pallas_call x0 -> x1, Pallas kernels: none -> 170 us  [one_step(): pl.pallas_call(functools.partial(step_kernel, names, groups, members, FOR...]
    all_to_all x6 -> x0, waiting for transfers between devices: 147 us -> none  [the longest x1 102 us: sent_and_summed(): lax.all_to_all(tiles, axis, split_axis=0, concat_axis=0, tiled=True)]
    all_gather x2 -> x0, waiting for transfers between devices: 146 us -> none  [the longest x1 74.4 us: local(): grad_cols_all = lax.all_gather(grad_cols, 'fsdp', axis=0, tiled=True)]
    all_to_all x6 -> x0, starting transfers between devices: 29.1 us -> none  [the longest x4 19.4 us: copy_for_each(): return lax.all_to_all(copies, axis, split_axis=0, concat_axis=0, tiled=True)]
    concatenate x2 -> x0, local copies, waits for them, and re-layouts: 13.8 us -> none  [the longest x1 8.43 us: column_section(): jnp.concatenate([matrix for triple in weight_sets for matrix in triple[:2...]
    reduce_sum x12 -> x0, other arithmetic: 10.6 us -> none  [the longest x3 6.15 us: sent_and_summed(): return arrived.sum(axis=0)]
    dot_general x6 -> x3, matrix products: 16.8 us -> 6.59 us  [outer(): lax.dot_general(left, right, (((0,), (0,)), ((), ())), preferred_element_...]
  transfers between devices with their start and end apart: 8 -> 0, of which waited for: 7 -> 0; matrix products, arithmetic and copies ran while one was open for 5% -> 0% of each run, Pallas kernels for 0% -> 0%
where the time goes in v1:
time: 178 us
  Pallas kernels  170 us (96%)
  matrix products  6.59 us (4%)
    pallas_call x1, Pallas kernels, one_step(): pl.pallas_call(functools.partial(step_kernel, names, groups, members, FOR...  170 us
    dot_general x3, matrix products, outer(): lax.dot_general(left, right, (((0,), (0,)), ((), ())), preferred_element_...  6.59 us

profile of v1, /device:TPU:1, one launch (start us, length us, event | category | flops | bytes accessed | tf_op | source)
XLA Modules:
  0.0 178.0 jit_solution(1445453922556890241)
XLA Ops:
  0.6 170.2 %one_step.1 = (bf16[1024,512]{1,0:T(8,128)(2,1)}, bf16[2,1024,462]{2,1,0:T(8,128)(2,1)}, bf16[1024,462]{1,0:T(8,128)(2,1)}, bf16[1024,512]{1,0:T(8,128)(2,1)}, f32[1,32]{1,0:T(1,128)}) custom-call(bf16[4,4096]{1,0:T(4,128)(2,1)} %refs_0_.1, f32[1,4096]{1,0:T(1,128)} %bitcast.20, s32[1,32]{1,0:T(1,128)} %refs_2_.1, s32[1,32]{1,0:T(1,128)} %refs_3_.1, ...), custom_call_target="tpu_custom_call" | custom-call | tf_op jit(solution)/shard_map/one_step/pallas_call | solution.py:667
  170.9 0.0 copy-start
  170.9 0.0 copy-start.1
  170.9 3.3 %fusion.6 = f32[462,512]{1,0:T(8,128)} fusion(bf16[1024,462]{1,0:T(8,128)(2,1)} %get-tuple-element.11, bf16[1024,512]{1,0:T(8,128)(2,1)} %get-tuple-element.12), kind=kOutput, calls=%fused_computation.6 | convolution fusion | flops 484442112 | bytes 2940928 | tf_op jit(solution)/shard_map/dot_general | solution.py:715
  174.2 0.0 copy-done
  174.2 0.0 copy-done.1
  174.2 1.6 fusion
  175.9 0.0 copy-start.2
  175.9 1.6 fusion.2
  177.5 0.0 copy-done.2
  177.5 0.5 copy.17
Async XLA Ops:
  170.9 3.3 %copy-start = (bf16[2,1024,462]{2,1,0:T(8,128)(2,1)S(1)}, bf16[2,1024,462]{2,1,0:T(8,128)(2,1)}, u32[]{:S(2)}) copy-start(bf16[2,1024,462]{2,1,0:T(8,128)(2,1)} %get-tuple-element.10) | copy-start | bytes 5677060
  170.9 3.3 %copy-start.1 = (bf16[1024,512]{1,0:T(8,128)(2,1)S(1)}, bf16[1024,512]{1,0:T(8,128)(2,1)}, u32[]{:S(2)}) copy-start(bf16[1024,512]{1,0:T(8,128)(2,1)} %get-tuple-element.9) | copy-start | bytes 3145732
  175.9 1.6 copy-start.2
